TPU v7x, 16 devices: a whole 2x2x2 slice. The times are simulated.
16 devices in a mesh: dp: 4 (over z, y), tp: 4 (over x, core).
Axes of the slice: x: 2, y: 2, z: 2, core: 2. Of those that a mesh axis runs over, the one named last changes fastest.
Arguments:
- x: bfloat16 [32, 128, 8192], P('dp'), parts along dimension 0
- seq_lens: int32 [32], P('dp'), parts along dimension 0
- w_query: bfloat16 [8192, 8192], P(None, 'tp')
- w_key: bfloat16 [8192, 1024], P(None, 'tp')
- w_value: bfloat16 [8192, 1024], P(None, 'tp')
- w_out: bfloat16 [8192, 8192], P('tp')
- w_gate: bfloat16 [8192, 22016], P(None, 'tp')
- w_up: bfloat16 [8192, 22016], P(None, 'tp')
- w_down: bfloat16 [22016, 8192], P('tp')
- attn_gain: bfloat16 [8192], replicated
- mlp_gain: bfloat16 [8192], replicated
- k_cache: bfloat16 [32, 256, 8, 128], P('dp', None, 'tp'), parts along dimension 0
- v_cache: bfloat16 [32, 256, 8, 128], P('dp', None, 'tp'), parts along dimension 0
Outputs:
- output 1: bfloat16 [32, 128, 8192], P('dp'), parts along dimension 0
- output 2: bfloat16 [32, 256, 8, 128], P('dp', None, 'tp'), parts along dimension 0
- output 3: bfloat16 [32, 256, 8, 128], P('dp', None, 'tp'), parts along dimension 0
There are 4 independent parts. A program takes and returns all parts, laid end to end along the dimension named above; an argument that names none is the same for every part.
All inputs are finite; a program needn't handle non-finite values.
Results may differ from a plain program's by a relative error of at most 0.0111989.
Values are sent between devices in bfloat16 or wider.
A program may use at most 1.5 GiB of HBM per device.

v0:
```python
import jax
import jax.numpy as jnp
from jax import lax
from jax.sharding import PartitionSpec as P

EPS = 1e-5
ROPE_BASE = 10000.0


def rms_norm(rows, gain):
    rows32 = rows.astype(jnp.float32)
    inv_rms = lax.rsqrt(jnp.mean(rows32 * rows32, axis=-1, keepdims=True) + EPS)
    return (rows32 * inv_rms * gain.astype(jnp.float32)).astype(jnp.bfloat16)


def rotary(vecs):
    seq_len = vecs.shape[1]
    head_dim = vecs.shape[-1]
    half_dim = head_dim // 2
    inv_freq = ROPE_BASE ** (-jnp.arange(0, head_dim, 2).astype(jnp.float32) / head_dim)
    angles = jnp.arange(seq_len).astype(jnp.float32)[:, None] * inv_freq[None, :]
    table_shape = (1, seq_len) + (1,) * (vecs.ndim - 3) + (half_dim,)
    cos_tab = jnp.cos(angles).reshape(table_shape)
    sin_tab = jnp.sin(angles).reshape(table_shape)
    pairs = vecs.reshape(vecs.shape[:-1] + (half_dim, 2))
    even_part = pairs[..., 0]
    odd_part = pairs[..., 1]
    turned = jnp.stack([even_part * cos_tab - odd_part * sin_tab, even_part * sin_tab + odd_part * cos_tab], axis=-1)
    return turned.reshape(vecs.shape).astype(jnp.bfloat16)


def causal_attention(queries, keys, values, seq_lens):
    seq_len = queries.shape[1]
    head_dim = queries.shape[-1]
    scores = jnp.einsum("bqkgh,bskh->bkgqs", queries, keys, preferred_element_type=jnp.float32) * head_dim ** -0.5
    positions = jnp.arange(seq_len)
    allowed = (positions[None, None, :] <= positions[None, :, None]) & (positions[None, None, :] < seq_lens[:, None, None])
    scores = jnp.where(allowed[:, None, None], scores, -jnp.inf)
    probs = jax.nn.softmax(scores, axis=-1).astype(jnp.bfloat16)
    return jnp.einsum("bkgqs,bskh->bqkgh", probs, values, preferred_element_type=jnp.float32).astype(jnp.bfloat16)


def sum_partials(partial, resid_rows, tp_size):
    batch_size, seq_len, model_width = partial.shape
    stacked = partial.reshape(batch_size, tp_size, seq_len // tp_size, model_width)
    received = lax.all_to_all(stacked, "tp", 1, 1, tiled=True)
    summed = jnp.sum(received.astype(jnp.float32), axis=1)
    return (resid_rows.astype(jnp.float32) + summed).astype(jnp.bfloat16)


def solution(mesh):
    tp_size = mesh.shape["tp"]

    def layer_shard(x, seq_lens, w_query, w_key, w_value, w_out, w_gate, w_up, w_down, attn_gain, mlp_gain, k_cache, v_cache):
        batch_size, seq_len, model_width = x.shape
        head_dim = k_cache.shape[3]
        kv_local = k_cache.shape[2]
        group_size = w_query.shape[1] // (head_dim * kv_local)
        rows_each = seq_len // tp_size
        tp_index = lax.axis_index("tp")
        normed = rms_norm(x, attn_gain)
        queries = rotary(jnp.einsum("bsd,dk->bsk", normed, w_query, preferred_element_type=jnp.float32).reshape(batch_size, seq_len, kv_local, group_size, head_dim))
        keys = rotary(jnp.einsum("bsd,dk->bsk", normed, w_key, preferred_element_type=jnp.float32).reshape(batch_size, seq_len, kv_local, head_dim))
        values = jnp.einsum("bsd,dk->bsk", normed, w_value, preferred_element_type=jnp.float32).astype(jnp.bfloat16).reshape(batch_size, seq_len, kv_local, head_dim)
        valid = (jnp.arange(seq_len)[None, :] < seq_lens[:, None])[:, :, None, None]
        keys = jnp.where(valid, keys, jnp.zeros_like(keys))
        values = jnp.where(valid, values, jnp.zeros_like(values))
        k_cache_out = lax.dynamic_update_slice(k_cache, keys, (0, 0, 0, 0))
        v_cache_out = lax.dynamic_update_slice(v_cache, values, (0, 0, 0, 0))
        attn_rows = causal_attention(queries, keys, values, seq_lens).reshape(batch_size, seq_len, -1)
        attn_part = jnp.einsum("bsk,kd->bsd", attn_rows, w_out, preferred_element_type=jnp.float32).astype(jnp.bfloat16)
        x_rows = lax.dynamic_slice_in_dim(x, tp_index * rows_each, rows_each, axis=1)
        hidden_rows = sum_partials(attn_part, x_rows, tp_size)
        normed_mlp = lax.all_gather(rms_norm(hidden_rows, mlp_gain), "tp", axis=1, tiled=True)
        gate_pre = jnp.einsum("bsd,df->bsf", normed_mlp, w_gate, preferred_element_type=jnp.float32)
        up_pre = jnp.einsum("bsd,df->bsf", normed_mlp, w_up, preferred_element_type=jnp.float32)
        gated = (jax.nn.silu(gate_pre) * up_pre).astype(jnp.bfloat16)
        mlp_part = jnp.einsum("bsf,fd->bsd", gated, w_down, preferred_element_type=jnp.float32).astype(jnp.bfloat16)
        out_rows = sum_partials(mlp_part, hidden_rows, tp_size)
        y = lax.all_gather(out_rows, "tp", axis=1, tiled=True)
        return y, k_cache_out, v_cache_out

    cache_spec = P("dp", None, "tp", None)
    return jax.shard_map(layer_shard, mesh=mesh, in_specs=(P("dp", None, None), P("dp"), P(None, "tp"), P(None, "tp"), P(None, "tp"), P("tp", None), P(None, "tp"), P(None, "tp"), P("tp", None), P(), P(), cache_spec, cache_spec), out_specs=(P("dp", None, None), cache_spec, cache_spec), check_vma=False)
```

profile of v0, /device:TPU:0, one launch (start us, length us, event | category | flops | bytes accessed | tf_op | source)
XLA Modules:
  0.0 1136.1 jit_solution(15945073317683410681)
XLA Ops:
  7.2 2.9 copy.68
  10.1 0.7 convert_element_type.109
  10.8 7.5 fusion.7
  18.3 8.3 fusion.25
  26.7 0.4 copy.33
  27.1 11.5 %fusion.43 = bf16[8,128,256]{2,1,0:T(8,128)(2,1)S(1)} fusion(bf16[8192,256]{1,0:T(8,128)(2,1)} %param.17, bf16[8,128,8192]{2,1,0:T(8,128)(2,1)} %param.13, f32[8192]{0:T(1024)S(1)} %convert_element_type.109, f32[8,128]{1,0:T(8,128)S(1)} %add_rsqrt_fusion.1), kind=kOutput, calls=%fused_computation.47 | convolution fusion | flops 4328783872 | bytes 21532672 | tf_op jit(solution)/shard_map/bsd,dk->bsk/dot_general | solution.py:64
  39.0 44.1 %fusion.12 = f32[8,128,2048]{2,1,0:T(8,128)} fusion(bf16[8192,2048]{1,0:T(8,128)(2,1)} %param.15, bf16[8,128,8192]{2,1,0:T(8,128)(2,1)} %param.13, f32[8192]{0:T(1024)S(1)} %convert_element_type.109, f32[8,128]{1,0:T(8,128)S(1)} %add_rsqrt_fusion.1), kind=kOutput, calls=%fused_computation.14 | convolution fusion | flops 34393292800 | bytes 58757120 | tf_op jit(solution)/shard_map/bsd,dk->bsk/dot_general | solution.py:62
  83.1 9.3 copy.34
  92.8 4.7 subtract_convert_fusion
  97.9 0.7 pad_maximum_fusion
  98.6 1.4 fusion.34
  100.0 4.6 fusion.53
  104.6 4.6 fusion.42
  109.3 41.5 %fusion.17 = bf16[8,128,8192]{2,1,0:T(8,128)(2,1)} fusion(bf16[8,128,2048]{1,2,0:T(8,128)(2,1)S(1)} %bitcast.74, bf16[2048,8192]{1,0:T(8,128)(2,1)} %param.18), kind=kOutput, calls=%fused_computation.20 | convolution fusion | flops 34368126976 | bytes 54525952 | tf_op jit(solution)/shard_map/bsk,kd->bsd/dot_general | solution.py:71
  150.8 13.9 %copy.41 = bf16[8,4,32,8192]{3,2,0,1:T(8,128)(2,1)} copy(bf16[8,4,32,8192]{3,2,1,0:T(8,128)(2,1)} %bitcast.68) | data formatting | bytes 33554432 | tf_op jit(solution)/shard_map/reshape | solution.py:45
  164.6 7.1 all-to-all-start
  171.8 183.6 %all-to-all-done = bf16[8,4,32,8192]{3,2,0,1:T(8,128)(2,1)} async-done(((bf16[8,4,32,8192]{3,2,0,1:T(8,128)(2,1)}), bf16[8,4,32,8192]{3,2,0,1:T(8,128)(2,1)}, u32[]{:S(2)}, u32[]{:S(2)}) %all-to-all-start) | async-done | bytes 16777248 | tf_op jit(solution)/shard_map/all_to_all | solution.py:46
  355.4 9.6 convert_reduce_fusion.1
  365.0 3.9 fusion.29
  368.9 2.0 copy-done
  370.9 3.2 fusion.31
  374.2 106.2 %all-gather.3.cloned.1.call-done = bf16[8,128,8192]{2,1,0:T(8,128)(2,1)} async-done(((bf16[8,32,8192]{2,1,0:T(8,128)(2,1)}), bf16[8,128,8192]{2,1,0:T(8,128)(2,1)}) %all-gather.3.cloned.1.call-update) | async-done | bytes 16777232 | tf_op jit(solution)/shard_map/all_gather | solution.py:74
  480.4 106.4 %fusion.5 = f32[8,128,5504]{2,1,0:T(8,128)} fusion(bf16[8,128,8192]{2,1,0:T(8,128)(2,1)} %all-gather.3.cloned.1.call-done, bf16[8192,5504]{1,0:T(8,128)(2,1)} %param.19), kind=kOutput, calls=%fused_computation.5 | convolution fusion | flops 92341796864 | bytes 129499136 | tf_op jit(solution)/shard_map/bsd,df->bsf/dot_general | solution.py:75
  586.8 109.2 %multiply_convert_fusion.clone.4 = bf16[8,128,5504]{2,1,0:T(8,128)(2,1)} fusion(f32[8,128,5504]{2,1,0:T(8,128)} %fusion.5, bf16[8,128,8192]{2,1,0:T(8,128)(2,1)} %all-gather.3.cloned.1.call-done, bf16[8192,5504]{1,0:T(8,128)(2,1)} %param.20), kind=kOutput, calls=%fused_computation.18.clone.clone.clone.1 | convolution fusion | flops 92375613440 | bytes 140771328 | tf_op jit(solution)/shard_map/bsd,df->bsf/dot_general | solution.py:76
  696.0 105.4 %fusion.14 = bf16[8,128,8192]{2,1,0:T(8,128)(2,1)} fusion(bf16[5504,8192]{1,0:T(8,128)(2,1)} %param.21, bf16[8,128,5504]{2,1,0:T(8,128)(2,1)} %multiply_convert_fusion.clone.4), kind=kOutput, calls=%fused_computation.19 | convolution fusion | flops 92350185472 | bytes 118226944 | tf_op jit(solution)/shard_map/bsf,fd->bsd/dot_general | solution.py:78
  801.4 8.6 copy.42
  810.0 186.1 %all_to_all.10 = bf16[8,4,32,8192]{3,2,0,1:T(8,128)(2,1)S(1)} all-to-all(bf16[8,4,32,8192]{3,2,0,1:T(8,128)(2,1)S(1)} %copy.42), channel_id=1, replica_groups=mesh['dp'=4,'tp'=4] {'tp'}, dimensions={1} | all-to-all | bytes 33554432 | tf_op jit(solution)/shard_map/all_to_all | solution.py:46
  996.1 6.8 convert_reduce_fusion
  1002.9 6.7 fusion.32
  1010.5 1.7 constant_dynamic-update-slice_fusion
  1012.2 102.7 %all-gather.5.cloned.1.call-done = bf16[8,128,8192]{2,1,0:T(8,128)(2,1)} async-done(((bf16[8,32,8192]{2,1,0:T(8,128)(2,1)}), bf16[8,128,8192]{2,1,0:T(8,128)(2,1)}) %all-gather.5.cloned.1.call-update) | async-done | bytes 16777232 | tf_op jit(solution)/shard_map/all_gather | solution.py:80
  1114.9 13.9 %copy.69 = bf16[8,128,8192]{2,1,0:T(8,128)(2,1)} copy(bf16[8,128,8192]{2,1,0:T(8,128)(2,1)} %all-gather.5.cloned.1.call-done) | data formatting | bytes 33554432
  (40 shorter events, 2.2 us)
Async XLA Ops:
  10.8 7.5 copy-start.9
  27.1 11.8 %copy-start.10 = (s32[8]{0:T(128)S(1)}, s32[8]{0:T(128)}, u32[]{:S(2)}) copy-start(s32[8]{0:T(128)} %param.14) | copy-start | bytes 100
  97.9 0.8 copy-start.2
  97.9 6.7 copy-start.4
  164.6 7.2 copy-start.8
  164.6 190.7 %all-to-all-start = ((bf16[8,4,32,8192]{3,2,0,1:T(8,128)(2,1)}), bf16[8,4,32,8192]{3,2,0,1:T(8,128)(2,1)}, u32[]{:S(2)}, u32[]{:S(2)}) async-start(bf16[8,4,32,8192]{3,2,0,1:T(8,128)(2,1)} %copy.41), calls=%async_computation | async-start | bytes 33554432 | tf_op jit(solution)/shard_map/all_to_all | solution.py:46
  171.7 308.6 %all-gather.3.cloned.1.call-start = ((), (), s32[]{:S(2)}) async-start(), calls=%async_computation.2 | async-start | bytes 20971520 | tf_op jit(solution)/shard_map/all_gather | solution.py:74
  368.9 2.1 copy-start
  374.2 740.8 %all-gather.5.cloned.1.call-start = ((), (), s32[]{:S(2)}) async-start(), calls=%async_computation.3 | async-start | bytes 20971520 | tf_op jit(solution)/shard_map/all_gather | solution.py:80
  996.1 6.8 copy-start.1
  1002.9 6.8 copy-start.3
  1002.9 7.2 copy-start.5
  1002.9 7.6 copy-start.7
  1012.2 116.7 %copy-start.6 = (bf16[8,256,2,128]{3,2,1,0:T(2,128)(2,1)}, bf16[8,256,2,128]{3,2,1,0:T(2,128)(2,1)S(1)}, u32[]{:S(2)}) copy-start(bf16[8,256,2,128]{3,2,1,0:T(2,128)(2,1)S(1)} %get-tuple-element.21) | copy-start | bytes 3145732
Sparse Core Ops, SparseCore 0:
  374.3 106.0 all-gather.2
  1009.7 105.1 all-gather.4
where the time goes:
time: 1140 us
  matrix products  432 us (38%)
  waiting for transfers between devices  392 us (34%)
  blocking collectives  186 us (16%)
  local copies, waits for them, and re-layouts  54.1 us (5%)
  other arithmetic  49.1 us (4%)
  between operations  14.8 us (1%)
    all_to_all x1, blocking collectives, sum_partials(): received = lax.all_to_all(stacked, 'tp', 1, 1, tiled=True)  186 us
    all_to_all x1, waiting for transfers between devices, sum_partials(): received = lax.all_to_all(stacked, 'tp', 1, 1, tiled=True)  184 us
    dot_general x1, matrix products, layer_shard(): jnp.einsum('bsd,df->bsf', normed_mlp, w_up, preferred_element_type=jnp.fl...  109 us
    dot_general x1, matrix products, layer_shard(): jnp.einsum('bsd,df->bsf', normed_mlp, w_gate, preferred_element_type=jnp....  106 us
    all_gather x1, waiting for transfers between devices, layer_shard(): lax.all_gather(rms_norm(hidden_rows, mlp_gain), 'tp', axis=1, tiled=True)  106 us
    dot_general x1, matrix products, layer_shard(): jnp.einsum('bsf,fd->bsd', gated, w_down, preferred_element_type=jnp.float32)  105 us
    all_gather x1, waiting for transfers between devices, layer_shard(): y = lax.all_gather(out_rows, 'tp', axis=1, tiled=True)  103 us
    dot_general x1, matrix products, layer_shard(): jnp.einsum('bsd,dk->bsk', normed, w_query, preferred_element_type=jnp.flo...  44.1 us
  transfers between devices with their start and end apart: 3, of which 3 were waited for; matrix products, arithmetic and copies ran while one was open for 0% of the time, Pallas kernels for 0%

commit v1 on v0

v1 whole, which is shorter than its diff:
```python
import functools

import jax
import jax.numpy as jnp
import numpy as np
from jax import lax
from jax.experimental import pallas as pl
from jax.experimental.pallas import tpu as pltpu
from jax.sharding import PartitionSpec as P

EPS = 1e-5
ROPE_BASE = 10000.0
VMEM_LIMIT = 63 * 1024 * 1024
TILE = 256
WIDE = 512
ANY = pl.BlockSpec(memory_space=pltpu.HBM)
ATTN_SEQS = (2, 2, 4)
OUT_PIECES = ((4, 4), (8,), (4, 4))
OUT_TILE = 1024
DOWN_PIECES = ((8, 8), (4, 4, 4, 4))


def kernel_call(kernel, **kwargs):
    return pl.pallas_call(kernel, **kwargs)


def dot32(lhs, rhs):
    return jnp.dot(lhs, rhs, preferred_element_type=jnp.float32)


def params():
    return pltpu.CompilerParams(dimension_semantics=("arbitrary",), vmem_limit_bytes=VMEM_LIMIT)


def once(shape, index=(0, 0)):
    return pl.BlockSpec(shape, lambda j, *_: index, pipeline_mode=pl.Buffered(1))


def attend_kernel(own, tiles_per_kv, first_seq, me_ref, lens_ref, x_ref, gain_ref, cos_ref, sin_ref, wq_ref, wk_ref, wv_ref, *rest):
    o_ref, k_ref, v_ref, normed, wbuf, sems = rest[-6:]
    step = pl.program_id(0)
    steps = pl.num_programs(0)
    me = me_ref[0]
    chunk = x_ref.shape[0]
    seq, head = cos_ref.shape
    seqs = chunk // seq

    def fetch(index, action):
        slot = lax.rem(index, 2)

        @pl.when(index == 0)
        def _():
            getattr(pltpu.make_async_copy(wk_ref, wbuf.at[slot], sems.at[slot]), action)()

        @pl.when(index == 1)
        def _():
            getattr(pltpu.make_async_copy(wv_ref, wbuf.at[slot], sems.at[slot]), action)()

        @pl.when((index >= 2) & (index < steps))
        def _():
            col = pl.multiple_of((index - 2) * TILE, TILE)
            getattr(pltpu.make_async_copy(wq_ref.at[:, pl.ds(col, TILE)], wbuf.at[slot], sems.at[slot]), action)()

    @pl.when(step == 0)
    def _():
        fetch(step, "start")

    fetch(step + 1, "start")

    @pl.when(step == 0)
    def _():
        gain = gain_ref[...].astype(jnp.float32)

        @pl.loop(0, chunk // 16)
        def _(r):
            at = pl.ds(pl.multiple_of(r * 16, 16), 16)
            rows = x_ref[at, :].astype(jnp.float32)
            inv = lax.rsqrt(jnp.mean(rows * rows, axis=-1, keepdims=True) + EPS)
            normed[at, :] = (rows * inv * gain).astype(jnp.bfloat16)

    fetch(step, "wait")

    def turn(vecs):
        even = lax.rem(lax.broadcasted_iota(jnp.int32, vecs.shape, 1), 2) == 0
        partner = jnp.where(even, pltpu.roll(vecs, head - 1, 1), pltpu.roll(vecs, 1, 1))
        return (vecs * cos_ref[...] + partner * sin_ref[...]).astype(jnp.bfloat16)

    proj = dot32(normed[...], wbuf[lax.rem(step, 2)])
    pos = lax.broadcasted_iota(jnp.int32, (seq, 1), 0)

    @pl.when(step == 0)
    def _():
        for s in range(seqs):
            for h in range(TILE // head):
                keys = turn(proj[s * seq:(s + 1) * seq, h * head:(h + 1) * head])
                k_ref[s * seq:(s + 1) * seq, h * head:(h + 1) * head] = jnp.where(pos < lens_ref[first_seq + s], keys, jnp.zeros_like(keys))

    @pl.when(step == 1)
    def _():
        for s in range(seqs):
            values = proj[s * seq:(s + 1) * seq].astype(jnp.bfloat16)
            v_ref[s * seq:(s + 1) * seq, :] = jnp.where(pos < lens_ref[first_seq + s], values, jnp.zeros_like(values))

    @pl.when(step >= 2)
    def _():
        kv_col = pl.multiple_of((step - 2) // tiles_per_kv * head, head)
        row_id = lax.broadcasted_iota(jnp.int32, (seq, seq), 0)
        col_id = lax.broadcasted_iota(jnp.int32, (seq, seq), 1)
        for s in range(seqs):
            at = slice(s * seq, (s + 1) * seq)
            keys = k_ref[at, pl.ds(kv_col, head)]
            values = v_ref[at, pl.ds(kv_col, head)]
            allowed = (col_id <= row_id) & (col_id < lens_ref[first_seq + s])
            for h in range(TILE // head):
                query = turn(proj[at, h * head:(h + 1) * head])
                scores = lax.dot_general(query, keys, (((1,), (1,)), ((), ())), preferred_element_type=jnp.float32) * head ** -0.5
                scores = jnp.where(allowed, scores, -jnp.inf)
                weights = jnp.exp(scores - jnp.max(scores, axis=-1, keepdims=True))
                probs = (weights / jnp.sum(weights, axis=-1, keepdims=True)).astype(jnp.bfloat16)
                mixed = dot32(probs, values).astype(jnp.bfloat16)
                for part in range(seq // own):
                    owner = s * (seq // own) + part
                    row = pl.multiple_of(lax.bitwise_xor(me, owner) * own, own)
                    o_ref[pl.ds(row, own), h * head:(h + 1) * head] = mixed[part * own:(part + 1) * own]


def attend(first_row, chunk, tp_size, me, lens, x_flat, gain, cos_tab, sin_tab, w_query, w_key, w_value, deps=()):
    width = x_flat.shape[1]
    seq, head = cos_tab.shape
    q_cols, kv_cols = w_query.shape[1], w_key.shape[1]
    steps = q_cols // TILE + 2
    x_spec = pl.BlockSpec((pl.Element(chunk), pl.Element(width)), lambda j, *_: (first_row, 0), pipeline_mode=pl.Buffered(1))
    return kernel_call(
        functools.partial(attend_kernel, chunk // tp_size, q_cols // TILE // (kv_cols // head), first_row // seq),
        grid_spec=pltpu.PrefetchScalarGridSpec(
            num_scalar_prefetch=2,
            grid=(steps,),
            in_specs=[x_spec, once((1, width)), once((seq, head)), once((seq, head))] + [ANY] * (3 + len(deps)),
            out_specs=[pl.BlockSpec((chunk, TILE), lambda j, *_: (0, jnp.maximum(j - 2, 0)))] + [pl.BlockSpec((chunk, kv_cols), lambda j, *_: (0, 0))] * 2,
            scratch_shapes=[pltpu.VMEM((chunk, width), jnp.bfloat16), pltpu.VMEM((2, width, TILE), jnp.bfloat16), pltpu.SemaphoreType.DMA((2,))],
        ),
        out_shape=[jax.ShapeDtypeStruct((chunk, q_cols), jnp.bfloat16)] + [jax.ShapeDtypeStruct((chunk, kv_cols), jnp.bfloat16)] * 2,
        compiler_params=params(),
    )(me, lens, x_flat, gain, cos_tab, sin_tab, w_query, w_key, w_value, *deps)


def load_lhs(blocks, lhs, sems, by_rows):
    @pl.when(pl.program_id(0) == 0)
    def _():
        copies, at = [], 0
        for i, block in enumerate(blocks):
            size = block.shape[0 if by_rows else 1]
            target = lhs.at[pl.ds(at, size)] if by_rows else lhs.at[:, pl.ds(at, size)]
            copies.append(pltpu.make_async_copy(block, target, sems.at[i]))
            at += size
        for copy in copies:
            copy.start()
        for copy in copies:
            copy.wait()


def gate_up_kernel(n_blocks, *refs):
    blocks, (wg_ref, wu_ref), (o_ref, lhs, sems) = refs[:n_blocks], refs[n_blocks:n_blocks + 2], refs[-3:]
    load_lhs(blocks, lhs, sems, True)
    gate = dot32(lhs[...], wg_ref[...])
    up = dot32(lhs[...], wu_ref[...])
    o_ref[...] = (gate * jax.nn.sigmoid(gate) * up).astype(jnp.bfloat16)


def gate_up(blocks, w_gate, w_up, first, tiles, deps=()):
    width = blocks[0].shape[1]
    rows = sum(block.shape[0] for block in blocks)
    cols = min(tiles * TILE, w_gate.shape[1] - first * TILE)
    w_spec = pl.BlockSpec((width, TILE), lambda j: (0, first + j))
    return kernel_call(
        functools.partial(gate_up_kernel, len(blocks)),
        grid=(tiles,),
        in_specs=[ANY] * len(blocks) + [w_spec] * 2 + [ANY] * len(deps),
        out_specs=pl.BlockSpec((rows, TILE), lambda j: (0, j)),
        out_shape=jax.ShapeDtypeStruct((rows, cols), jnp.bfloat16),
        scratch_shapes=[pltpu.VMEM((rows, width), jnp.bfloat16), pltpu.SemaphoreType.DMA((len(blocks),))],
        compiler_params=params(),
    )(*blocks, w_gate, w_up, *deps)


def project_kernel(n_blocks, n_outs, *refs):
    blocks, w_ref = refs[:n_blocks], refs[n_blocks]
    outs, lhs, sems = refs[-2 - n_outs:-2], refs[-2], refs[-1]
    load_lhs(blocks, lhs, sems, False)
    partial = dot32(lhs[...], w_ref[...]).astype(jnp.bfloat16)
    own = outs[0].shape[0]
    for k, out in enumerate(outs):
        out[...] = partial[k * own:(k + 1) * own]


def project(blocks, weight, tile, first, tiles, n_outs, deps=()):
    rows = blocks[0].shape[0]
    depth = weight.shape[0]
    own = rows // n_outs
    return kernel_call(
        functools.partial(project_kernel, len(blocks), n_outs),
        grid=(tiles,),
        in_specs=[ANY] * len(blocks) + [pl.BlockSpec((depth, tile), lambda j: (0, first + j))] + [ANY] * len(deps),
        out_specs=[pl.BlockSpec((own, tile), lambda j: (0, j))] * n_outs,
        out_shape=[jax.ShapeDtypeStruct((own, tiles * tile), jnp.bfloat16)] * n_outs,
        scratch_shapes=[pltpu.VMEM((rows, depth), jnp.bfloat16), pltpu.SemaphoreType.DMA((len(blocks),))],
        compiler_params=params(),
    )(*blocks, weight, *deps)


def add_norm_kernel(n_pieces, n_parts, *refs):
    pieces = [refs[p * n_parts:(p + 1) * n_parts] for p in range(n_pieces)]
    x_ref, gain_ref = refs[n_pieces * n_parts:n_pieces * n_parts + 2]
    h_ref, n_ref, h32 = refs[-3:]
    col = 0
    square = jnp.zeros((h_ref.shape[0], 1), jnp.float32)
    for parts in pieces:
        at = slice(col, col + parts[0].shape[1])
        total = parts[0][...].astype(jnp.float32)
        for part in parts[1:]:
            total = total + part[...].astype(jnp.float32)
        hidden = (x_ref[:, at].astype(jnp.float32) + total).astype(jnp.bfloat16)
        h_ref[:, at] = hidden
        hidden = hidden.astype(jnp.float32)
        h32[:, at] = hidden
        square = square + jnp.sum(hidden * hidden, axis=-1, keepdims=True)
        col += parts[0].shape[1]
    inv = lax.rsqrt(square / h_ref.shape[1] + EPS)
    n_ref[...] = (h32[...] * inv * gain_ref[...].astype(jnp.float32)).astype(jnp.bfloat16)


def add_norm(pieces, row_block, x_flat, gain, hidden, hidden_rows, hidden_first, deps=()):
    n_parts = len(pieces[0])
    own = pieces[0][0].shape[0]
    width = x_flat.shape[1]
    flat = [part for parts in pieces for part in parts]
    n_in = len(flat) + 2
    step_rows = 32
    steps = own // step_rows
    extra = (() if hidden is None else (hidden,)) + tuple(deps)

    def kernel(*refs):
        add_norm_kernel(len(pieces), n_parts, *refs[1:1 + n_in], *refs[1 + n_in + len(extra):])

    return kernel_call(
        kernel,
        grid_spec=pltpu.PrefetchScalarGridSpec(
            num_scalar_prefetch=1,
            grid=(steps,),
            in_specs=[pl.BlockSpec((step_rows, part.shape[1]), lambda j, *_: (j, 0)) for part in flat]
            + [pl.BlockSpec((step_rows, width), lambda j, at: (at[0] + j, 0)), once((1, width))] + [ANY] * len(extra),
            out_specs=[pl.BlockSpec((step_rows, width), lambda j, *_: (hidden_first // step_rows + j, 0)), pl.BlockSpec((step_rows, width), lambda j, *_: (j, 0))],
            scratch_shapes=[pltpu.VMEM((step_rows, width), jnp.float32)],
        ),
        out_shape=[jax.ShapeDtypeStruct((hidden_rows, width), jnp.bfloat16), jax.ShapeDtypeStruct((own, width), jnp.bfloat16)],
        input_output_aliases={} if hidden is None else {1 + n_in: 0},
        compiler_params=params(),
    )(row_block * steps, *flat, x_flat, gain, *extra)


def hold(arrays, deps):
    def kernel(*refs):
        pass

    return kernel_call(
        kernel,
        in_specs=[ANY] * (len(arrays) + len(deps)),
        out_specs=[ANY] * len(arrays),
        out_shape=[jax.ShapeDtypeStruct(a.shape, a.dtype) for a in arrays],
        input_output_aliases={i: i for i in range(len(arrays))},
    )(*arrays, *deps)


def add_rows(parts, hidden, first_col, deps=()):
    own, cols = parts[0].shape
    step_rows = 64

    def kernel(*refs):
        total = refs[0][...].astype(jnp.float32)
        for ref in refs[1:len(parts)]:
            total = total + ref[...].astype(jnp.float32)
        refs[-1][...] = (refs[len(parts)][...].astype(jnp.float32) + total).astype(jnp.bfloat16)

    spec = pl.BlockSpec((step_rows, cols), lambda i: (i, 0))
    return kernel_call(
        kernel,
        grid=(own // step_rows,),
        in_specs=[spec] * len(parts) + [pl.BlockSpec((step_rows, cols), lambda i: (i, first_col // cols))] + [ANY] * len(deps),
        out_specs=spec,
        out_shape=jax.ShapeDtypeStruct((own, cols), jnp.bfloat16),
        compiler_params=params(),
    )(*parts, hidden, *deps)


def place_rows(me, y, shape, blocks, row_block, first_col, part, deps=()):
    parts = blocks[0].shape[0] // part
    cols = blocks[0].shape[1]

    def kernel(*refs):
        for k in range(len(blocks)):
            @pl.when(pl.program_id(0) == k)
            def _():
                refs[-2][...] = refs[1 + k][...]

        refs[-1][...] = jnp.zeros_like(refs[-1])

    block = (part, cols)
    return kernel_call(
        kernel,
        grid_spec=pltpu.PrefetchScalarGridSpec(
            num_scalar_prefetch=1,
            grid=(len(blocks), parts),
            in_specs=[pl.BlockSpec(block, lambda b, i, me, k=k: (jnp.where(b == k, i, jnp.where(b < k, 0, parts - 1)), 0)) for k in range(len(blocks))] + [ANY] * (len(deps) + (y is not None)),
            out_specs=[pl.BlockSpec(block, lambda b, i, me: (row_block(lax.bitwise_xor(me[0], b), i), first_col // cols)), pl.BlockSpec((8, 128), lambda *_: (0, 0))],
        ),
        out_shape=[jax.ShapeDtypeStruct(shape, jnp.bfloat16), jax.ShapeDtypeStruct((8, 128), jnp.float32)],
        input_output_aliases={} if y is None else {1 + len(blocks): 0},
        compiler_params=pltpu.CompilerParams(dimension_semantics=("arbitrary",) * 2, vmem_limit_bytes=VMEM_LIMIT),
    )(me, *blocks, *(() if y is None else (y,)), *deps)


def rotary_tables(seq_len, head_dim):
    inv_freq = np.float32(ROPE_BASE) ** (-np.arange(0, head_dim, 2, dtype=np.float32) / np.float32(head_dim))
    angles = (np.arange(seq_len, dtype=np.float32)[:, None] * inv_freq[None, :].astype(np.float32)).astype(np.float64)
    sign = np.where(np.arange(head_dim) % 2 == 0, -1.0, 1.0)[None, :]
    return np.repeat(np.cos(angles), 2, axis=1).astype(np.float32), (np.repeat(np.sin(angles), 2, axis=1) * sign).astype(np.float32)


def solution(mesh):
    tp_size = mesh.shape["tp"]

    def swap(block, mask):
        return lax.ppermute(block, "tp", [(s, s ^ mask) for s in range(tp_size)])

    def exchange(pieces):
        return [pieces[0]] + [swap(pieces[k], k) for k in (2, 3, 1)]

    def send(block):
        return block, swap(block, 1), swap(block, 2)

    def forward(sent, deps):
        block, from_core, from_chip = sent
        from_chip = hold([from_chip], deps)[0]
        return [block, from_core, from_chip, swap(from_chip, 1)]

    def layer_body(x, seq_lens, w_query, w_key, w_value, w_out, w_gate, w_up, w_down, attn_gain, mlp_gain, k_cache, v_cache):
        batch_size, seq_len, width = x.shape
        head_dim = k_cache.shape[3]
        rows = batch_size * seq_len
        x_flat = x.reshape(rows, width)
        me = lax.axis_index("tp").astype(jnp.int32).reshape(1)
        cos_tab, sin_tab = (jnp.asarray(t) for t in rotary_tables(seq_len, head_dim))
        gain1, gain2 = attn_gain.reshape(1, width), mlp_gain.reshape(1, width)
        starts = [sum(ATTN_SEQS[:c]) * seq_len for c in range(len(ATTN_SEQS))]
        sizes = [n * seq_len for n in ATTN_SEQS]
        owns = [n // tp_size for n in sizes]

        def attn(c, deps=()):
            return attend(starts[c], sizes[c], tp_size, me, seq_lens, x_flat, gain1, cos_tab, sin_tab, w_query, w_key, w_value, deps)

        def pieces_of(lhs, weight, tile, tiles, deps=()):
            out, first = [], 0
            for n in tiles:
                out.append(project(lhs, weight, tile, first, n, tp_size, deps))
                deps = (out[-1][0],)
                first += n
            return out

        def out_proj(c, lhs, deps=()):
            return pieces_of([lhs], w_out, OUT_TILE, OUT_PIECES[c], deps)

        def norm(c, received, hidden, hidden_rows, hidden_first, deps):
            return add_norm(received, starts[c] // owns[c] + me, x_flat, gain2, hidden, hidden_rows, hidden_first, deps)

        o0, k0, v0 = attn(0)
        p0 = out_proj(0, o0)
        r0 = [exchange(p) for p in p0]
        o1, k1, v1 = attn(1, (p0[-1][0],))
        h0, n0 = norm(0, r0, None, owns[0] + owns[1], 0, (o1,))
        g0 = send(n0)
        p1 = out_proj(1, o1, (n0,))
        r1 = [exchange(p) for p in p1]
        o2, k2, v2 = attn(2, (p1[-1][0],))
        h0, n1 = norm(1, r1, h0, owns[0] + owns[1], owns[0], (o2,))
        g1 = send(n1)
        g0 = forward(g0, (n1,))
        p2 = out_proj(2, o2, (g0[2],))
        r2 = [exchange(p) for p in p2]
        g1 = forward(g1, (p2[-1][0],))
        lhs0 = [g[k] for k in range(tp_size) for g in (g0, g1)]
        all_tiles = -(-w_gate.shape[1] // TILE)
        half = all_tiles // 2
        u0 = [gate_up(lhs0, w_gate, w_up, 0, all_tiles, (g1[2],))]
        h1, n2 = norm(2, r2, None, owns[2], 0, (u0[0],))
        g2 = send(n2)
        d0 = pieces_of(u0, w_down, WIDE, DOWN_PIECES[0], (n2,))
        s0 = [exchange(p) for p in d0]
        g2 = forward(g2, (d0[-1][0],))
        u1 = [gate_up(g2, w_gate, w_up, 0, half, (g2[2],))]

        def add(c, i, received, hidden, deps):
            first = sum(DOWN_PIECES[c][:i]) * WIDE
            return add_rows(received[i], hidden, first, deps)

        a00 = add(0, 0, s0, h0, (u1[0],))
        e00 = send(a00)
        u1.append(gate_up(g2, w_gate, w_up, half, all_tiles - half, (a00,)))
        a01 = add(0, 1, s0, h0, (u1[1],))
        e01 = send(a01)
        d1 = pieces_of(u1, w_down, WIDE, DOWN_PIECES[1], (a01,))
        s1 = [exchange(p) for p in d1]

        def row_block(c):
            return (lambda owner, i: tp_size * i + owner) if c == 0 else (lambda owner, i: starts[2] // owns[2] + owner)

        def place(c, i, y, blocks, deps):
            first = sum(DOWN_PIECES[c][:i]) * WIDE
            return place_rows(me, y, (rows, width), blocks, row_block(c), first, owns[0] if c == 0 else owns[2], deps)

        def cache_of(cache, blocks):
            new_rows = jnp.concatenate(blocks, axis=0).reshape(batch_size, seq_len, -1, head_dim)
            return jnp.concatenate([new_rows, cache[:, seq_len:]], axis=1)

        k_out, v_out = cache_of(k_cache, [k0, k1, k2]), cache_of(v_cache, [v0, v1, v2])
        b00 = forward(e00, (d1[-1][0],))
        a10 = add(1, 0, s1, h1, (b00[2],))
        e10 = send(a10)
        b01 = forward(e01, (a10,))
        a11 = add(1, 1, s1, h1, (b01[2],))
        e11 = send(a11)
        y, token = place(0, 0, None, b00, (a11,))
        b10 = forward(e10, (token, k_out, v_out))
        a12 = add(1, 2, s1, h1, (b10[2],))
        e12 = send(a12)
        y, token = place(0, 1, y, b01, (a12,))
        b11 = forward(e11, (token,))
        y, token = place(1, 0, y, b10, (b11[2],))
        a13 = add(1, 3, s1, h1, (token,))
        e13 = send(a13)
        y, token = place(1, 1, y, b11, (a13,))
        b12 = forward(e12, (token,))
        b13 = forward(e13, (b12[2],))
        y, token = place(1, 2, y, b12, (b13[2],))
        y, token = place(1, 3, y, b13, ())

        return y.reshape(x.shape), k_out, v_out

    cache_spec = P("dp", None, "tp", None)
    return jax.shard_map(layer_body, mesh=mesh, in_specs=(P("dp", None, None), P("dp"), P(None, "tp"), P(None, "tp"), P(None, "tp"), P("tp", None), P(None, "tp"), P(None, "tp"), P("tp", None), P(), P(), cache_spec, cache_spec), out_specs=(P("dp", None, None), cache_spec, cache_spec), check_vma=False)
```

time: 1140 us -> 799 us (0.70)
  Pallas kernels: 0 us -> 629 us
  matrix products: 432 us -> 0 us
  waiting for transfers between devices: 392 us -> 106 us
  blocking collectives: 186 us -> 0 us
  local copies, waits for them, and re-layouts: 54.1 us -> 5.22 us
  other arithmetic: 49.1 us -> 6.88 us
  starting transfers between devices: 7.18 us -> 41.4 us
  between operations: 14.8 us -> 1.34 us
    pallas_call x0 -> x41, Pallas kernels: none -> 629 us  [the longest x3 228 us: gate_up(): kernel_call(functools.partial(gate_up_kernel, len(blocks)), grid=(tiles,)...]
    dot_general x9 -> x0, matrix products: 432 us -> none  [the longest x1 109 us: layer_shard(): jnp.einsum('bsd,df->bsf', normed_mlp, w_up, preferred_element_type=jnp.fl...]
    all_gather x2 -> x0, waiting for transfers between devices: 209 us -> none  [the longest x1 106 us: layer_shard(): lax.all_gather(rms_norm(hidden_rows, mlp_gain), 'tp', axis=1, tiled=True)]
    all_to_all x1 -> x0, blocking collectives: 186 us -> none  [sum_partials(): received = lax.all_to_all(stacked, 'tp', 1, 1, tiled=True)]
    all_to_all x1 -> x0, waiting for transfers between devices: 184 us -> none  [sum_partials(): received = lax.all_to_all(stacked, 'tp', 1, 1, tiled=True)]
    ppermute x0 -> x60, waiting for transfers between devices: none -> 106 us  [swap(): return lax.ppermute(block, 'tp', [(s, s ^ mask) for s in range(tp_size)])]
    ppermute x0 -> x60, starting transfers between devices: none -> 41.4 us  [swap(): return lax.ppermute(block, 'tp', [(s, s ^ mask) for s in range(tp_size)])]
    reduce_sum x4 -> x0, other arithmetic: 27.7 us -> none  [the longest x2 16.4 us: sum_partials(): summed = jnp.sum(received.astype(jnp.float32), axis=1)]
  transfers between devices with their start and end apart: 3 -> 60, of which waited for: 3 -> 11; matrix products, arithmetic and copies ran while one was open for 0% -> 1% of each run, Pallas kernels for 0% -> 68%
where the time goes in v1:
time: 799 us; the launch traced here: 790 us
  Pallas kernels  629 us (79%)
  waiting for transfers between devices  106 us (13%)
  starting transfers between devices  41.4 us (5%)
    pallas_call x3, Pallas kernels, gate_up(): kernel_call(functools.partial(gate_up_kernel, len(blocks)), grid=(tiles,)...  228 us
    pallas_call x11, Pallas kernels, project(): kernel_call(functools.partial(project_kernel, len(blocks), n_outs), grid=...  213 us
    pallas_call x3, Pallas kernels, attend(): kernel_call(functools.partial(attend_kernel, chunk // tp_size, q_cols //...  126 us
    ppermute x60, waiting for transfers between devices, swap(): return lax.ppermute(block, 'tp', [(s, s ^ mask) for s in range(tp_size)])  106 us
    ppermute x60, starting transfers between devices, swap(): return lax.ppermute(block, 'tp', [(s, s ^ mask) for s in range(tp_size)])  41.4 us
    pallas_call x6, Pallas kernels, place_rows(): kernel_call(kernel, grid_spec=pltpu.PrefetchScalarGridSpec(num_scalar_pre...  28.4 us
    pallas_call x6, Pallas kernels, add_rows(): kernel_call(kernel, grid=(own // step_rows,), in_specs=[spec] * len(parts...  17.4 us
    pallas_call x3, Pallas kernels, add_norm(): kernel_call(kernel, grid_spec=pltpu.PrefetchScalarGridSpec(num_scalar_pre...  16 us
  transfers between devices with their start and end apart: 60, of which 11 were waited for; matrix products, arithmetic and copies ran while one was open for 1% of the time, Pallas kernels for 68%

profile of v1, /device:TPU:0, one launch (start us, length us, event | category | flops | bytes accessed | tf_op | source)
XLA Modules:
  0.0 789.5 jit_solution(2091104846824139442)
XLA Ops:
  2.0 33.5 %shard_map.166 = (bf16[256,2048]{1,0:T(8,128)(2,1)}, bf16[256,256]{1,0:T(8,128)(2,1)}, bf16[256,256]{1,0:T(8,128)(2,1)}) custom-call(s32[1]{0:T(128)} %bitcast.me_ref.refs_0_, s32[8]{0:T(128)} %lens_ref.5, bf16[1024,8192]{1,0:T(8,128)(2,1)} %bitcast.3, bf16[1,8192]{1,0:T(2,128)(2,1)} %reshape.29.gain_ref, f32[128,128]{1,0:T(8,128)} %constant.12.clone.cos_ref, ...), custom_call_target="tpu_custom_call" | custom-call | tf_op jit(solution)/shard_map/pallas_call | solution.py:133
  35.4 11.2 %shard_map.167 = (bf16[64,4096]{1,0:T(8,128)(2,1)}, bf16[64,4096]{1,0:T(8,128)(2,1)}, bf16[64,4096]{1,0:T(8,128)(2,1)}, bf16[64,4096]{1,0:T(8,128)(2,1)}) custom-call(bf16[256,2048]{1,0:T(8,128)(2,1)} %get-tuple-element.72.refs_0_, bf16[2048,8192]{1,0:T(8,128)(2,1)} %refs_1_.11), custom_call_target="tpu_custom_call" | custom-call | tf_op jit(solution)/shard_map/pallas_call | solution.py:200
  46.7 11.2 %shard_map.168 = (bf16[64,4096]{1,0:T(8,128)(2,1)}, bf16[64,4096]{1,0:T(8,128)(2,1)}, bf16[64,4096]{1,0:T(8,128)(2,1)}, bf16[64,4096]{1,0:T(8,128)(2,1)}) custom-call(bf16[256,2048]{1,0:T(8,128)(2,1)} %get-tuple-element.72.refs_0_, bf16[2048,8192]{1,0:T(8,128)(2,1)} %refs_1_.11, bf16[64,4096]{1,0:T(8,128)(2,1)} %get-tuple-element.73.refs_2_.refs_1_), custom_call_target="tpu_custom_call" | custom-call | tf_op jit(solution)/shard_map/pallas_call | solution.py:200
  63.3 10.8 %collective-permute-done.3.refs_6_ = bf16[64,4096]{1,0:T(8,128)(2,1)S(1)} collective-permute-done((bf16[64,4096]{1,0:T(8,128)(2,1)}, bf16[64,4096]{1,0:T(8,128)(2,1)S(1)}, u32[]{:S(2)}, u32[]{:S(2)}) %collective-permute-start.3) | collective-permute-done | bytes 524320 | tf_op jit(solution)/shard_map/ppermute | solution.py:333
  74.2 33.6 %shard_map.169 = (bf16[256,2048]{1,0:T(8,128)(2,1)}, bf16[256,256]{1,0:T(8,128)(2,1)}, bf16[256,256]{1,0:T(8,128)(2,1)}) custom-call(s32[1]{0:T(128)} %bitcast.me_ref.refs_0_, s32[8]{0:T(128)} %lens_ref.5, bf16[1024,8192]{1,0:T(8,128)(2,1)} %bitcast.4, bf16[1,8192]{1,0:T(2,128)(2,1)} %reshape.29.gain_ref, f32[128,128]{1,0:T(8,128)} %constant.12.clone.cos_ref, ...), custom_call_target="tpu_custom_call" | custom-call | tf_op jit(solution)/shard_map/pallas_call | solution.py:133
  108.4 4.1 shard_map.170
  112.6 18.8 %shard_map.171 = (bf16[64,8192]{1,0:T(8,128)(2,1)}, bf16[64,8192]{1,0:T(8,128)(2,1)}, bf16[64,8192]{1,0:T(8,128)(2,1)}, bf16[64,8192]{1,0:T(8,128)(2,1)}) custom-call(bf16[256,2048]{1,0:T(8,128)(2,1)} %get-tuple-element.75.refs_11_.refs_0_, bf16[2048,8192]{1,0:T(8,128)(2,1)} %refs_1_.11, bf16[64,8192]{1,0:T(8,128)(2,1)} %get-tuple-element.82.refs_2_.refs_0_), custom_call_target="tpu_custom_call" | custom-call | tf_op jit(solution)/shard_map/pallas_call | solution.py:200
  135.6 59.3 %shard_map.172 = (bf16[512,2048]{1,0:T(8,128)(2,1)}, bf16[512,256]{1,0:T(8,128)(2,1)}, bf16[512,256]{1,0:T(8,128)(2,1)}) custom-call(s32[1]{0:T(128)} %bitcast.me_ref.refs_0_, s32[8]{0:T(128)} %lens_ref.5, bf16[1024,8192]{1,0:T(8,128)(2,1)} %bitcast.6, bf16[1,8192]{1,0:T(2,128)(2,1)} %reshape.29.gain_ref, f32[128,128]{1,0:T(8,128)} %constant.12.clone.cos_ref, ...), custom_call_target="tpu_custom_call" | custom-call | tf_op jit(solution)/shard_map/pallas_call | solution.py:133
  195.0 4.6 shard_map.173
  202.7 14.7 %shard_map.175 = (bf16[128,4096]{1,0:T(8,128)(2,1)}, bf16[128,4096]{1,0:T(8,128)(2,1)}, bf16[128,4096]{1,0:T(8,128)(2,1)}, bf16[128,4096]{1,0:T(8,128)(2,1)}) custom-call(bf16[512,2048]{1,0:T(8,128)(2,1)} %get-tuple-element.84.refs_8_.refs_0_, bf16[2048,8192]{1,0:T(8,128)(2,1)} %refs_1_.11, bf16[64,8192]{1,0:T(8,128)(2,1)} %shard_map.174.refs_2_.refs_4_), custom_call_target="tpu_custom_call" | custom-call | tf_op jit(solution)/shard_map/pallas_call | solution.py:200
  218.0 14.8 %shard_map.176 = (bf16[128,4096]{1,0:T(8,128)(2,1)}, bf16[128,4096]{1,0:T(8,128)(2,1)}, bf16[128,4096]{1,0:T(8,128)(2,1)}, bf16[128,4096]{1,0:T(8,128)(2,1)}) custom-call(bf16[512,2048]{1,0:T(8,128)(2,1)} %get-tuple-element.84.refs_8_.refs_0_, bf16[2048,8192]{1,0:T(8,128)(2,1)} %refs_1_.11, bf16[128,4096]{1,0:T(8,128)(2,1)} %get-tuple-element.90.refs_2_.refs_1_), custom_call_target="tpu_custom_call" | custom-call | tf_op jit(solution)/shard_map/pallas_call | solution.py:200
  237.1 22.1 %collective-permute-done.13.refs_6_ = bf16[128,4096]{1,0:T(8,128)(2,1)} collective-permute-done((bf16[128,4096]{1,0:T(8,128)(2,1)}, bf16[128,4096]{1,0:T(8,128)(2,1)}, u32[]{:S(2)}, u32[]{:S(2)}) %collective-permute-start.13) | collective-permute-done | bytes 1048608 | tf_op jit(solution)/shard_map/ppermute | solution.py:333
  261.4 109.3 %shard_map.178.refs_11_.refs_0_ = bf16[512,5504]{1,0:T(8,128)(2,1)} custom-call(bf16[64,8192]{1,0:T(8,128)(2,1)} %get-tuple-element.82.refs_2_.refs_0_, bf16[64,8192]{1,0:T(8,128)(2,1)} %get-tuple-element.89.refs_1_, bf16[64,8192]{1,0:T(8,128)(2,1)} %collective-permute-done.16.refs_2_, bf16[64,8192]{1,0:T(8,128)(2,1)} %collective-permute-done.17.refs_3_, ...), custom_call_target="tpu_custom_call" | custom-call | tf_op jit(solution)/shard_map/pallas_call | solution.py:175
  370.7 7.2 shard_map.179
  378.1 32.1 %shard_map.180 = (bf16[128,4096]{1,0:T(8,128)(2,1)}, bf16[128,4096]{1,0:T(8,128)(2,1)}, bf16[128,4096]{1,0:T(8,128)(2,1)}, bf16[128,4096]{1,0:T(8,128)(2,1)}) custom-call(bf16[512,5504]{1,0:T(8,128)(2,1)} %shard_map.178.refs_11_.refs_0_, bf16[5504,8192]{1,0:T(8,128)(2,1)} %refs_2_.7, bf16[128,8192]{1,0:T(8,128)(2,1)} %get-tuple-element.98.refs_2_.refs_0_), custom_call_target="tpu_custom_call" | custom-call | tf_op jit(solution)/shard_map/pallas_call | solution.py:200
  410.1 32.2 %shard_map.181 = (bf16[128,4096]{1,0:T(8,128)(2,1)}, bf16[128,4096]{1,0:T(8,128)(2,1)}, bf16[128,4096]{1,0:T(8,128)(2,1)}, bf16[128,4096]{1,0:T(8,128)(2,1)}) custom-call(bf16[512,5504]{1,0:T(8,128)(2,1)} %shard_map.178.refs_11_.refs_0_, bf16[5504,8192]{1,0:T(8,128)(2,1)} %refs_2_.7, bf16[128,4096]{1,0:T(8,128)(2,1)} %get-tuple-element.99.refs_2_.refs_0_), custom_call_target="tpu_custom_call" | custom-call | tf_op jit(solution)/shard_map/pallas_call | solution.py:200
  445.0 24.2 %collective-permute-done.24.refs_1_ = bf16[128,4096]{1,0:T(8,128)(2,1)} collective-permute-done((bf16[128,4096]{1,0:T(8,128)(2,1)}, bf16[128,4096]{1,0:T(8,128)(2,1)}, u32[]{:S(2)}, u32[]{:S(2)}) %collective-permute-start.24) | collective-permute-done | bytes 1048608 | tf_op jit(solution)/shard_map/ppermute | solution.py:333
  471.3 59.2 %shard_map.183.refs_5_.refs_0_ = bf16[512,2816]{1,0:T(8,128)(2,1)} custom-call(bf16[128,8192]{1,0:T(8,128)(2,1)} %get-tuple-element.98.refs_2_.refs_0_, bf16[128,8192]{1,0:T(8,128)(2,1)} %collective-permute-done.21.refs_1_, bf16[128,8192]{1,0:T(8,128)(2,1)} %shard_map.182.refs_2_.refs_6_, bf16[128,8192]{1,0:T(8,128)(2,1)} %collective-permute-done.23.refs_3_, ...), custom_call_target="tpu_custom_call" | custom-call | tf_op jit(solution)/shard_map/pallas_call | solution.py:175
  530.6 3.6 shard_map.184.refs_6_.refs_1_
  536.2 59.2 %shard_map.185.refs_5_.refs_1_ = bf16[512,2688]{1,0:T(8,128)(2,1)} custom-call(bf16[128,8192]{1,0:T(8,128)(2,1)} %get-tuple-element.98.refs_2_.refs_0_, bf16[128,8192]{1,0:T(8,128)(2,1)} %collective-permute-done.21.refs_1_, bf16[128,8192]{1,0:T(8,128)(2,1)} %shard_map.182.refs_2_.refs_6_, bf16[128,8192]{1,0:T(8,128)(2,1)} %collective-permute-done.23.refs_3_, ...), custom_call_target="tpu_custom_call" | custom-call | tf_op jit(solution)/shard_map/pallas_call | solution.py:175
  595.4 3.6 shard_map.186.refs_3_.refs_1_
  599.0 19.4 %shard_map.187 = (bf16[128,2048]{1,0:T(8,128)(2,1)}, bf16[128,2048]{1,0:T(8,128)(2,1)}, bf16[128,2048]{1,0:T(8,128)(2,1)}, bf16[128,2048]{1,0:T(8,128)(2,1)}) custom-call(bf16[512,2816]{1,0:T(8,128)(2,1)} %shard_map.183.refs_5_.refs_0_, bf16[512,2688]{1,0:T(8,128)(2,1)} %shard_map.185.refs_5_.refs_1_, bf16[5504,8192]{1,0:T(8,128)(2,1)} %refs_2_.7, ...), custom_call_target="tpu_custom_call" | custom-call | tf_op jit(solution)/shard_map/pallas_call | solution.py:200
  620.7 19.5 %shard_map.188 = (bf16[128,2048]{1,0:T(8,128)(2,1)}, bf16[128,2048]{1,0:T(8,128)(2,1)}, bf16[128,2048]{1,0:T(8,128)(2,1)}, bf16[128,2048]{1,0:T(8,128)(2,1)}) custom-call(bf16[512,2816]{1,0:T(8,128)(2,1)} %shard_map.183.refs_5_.refs_0_, bf16[512,2688]{1,0:T(8,128)(2,1)} %shard_map.185.refs_5_.refs_1_, bf16[5504,8192]{1,0:T(8,128)(2,1)} %refs_2_.7, ...), custom_call_target="tpu_custom_call" | custom-call | tf_op jit(solution)/shard_map/pallas_call | solution.py:200
  644.8 19.5 %shard_map.189 = (bf16[128,2048]{1,0:T(8,128)(2,1)}, bf16[128,2048]{1,0:T(8,128)(2,1)}, bf16[128,2048]{1,0:T(8,128)(2,1)}, bf16[128,2048]{1,0:T(8,128)(2,1)}) custom-call(bf16[512,2816]{1,0:T(8,128)(2,1)} %shard_map.183.refs_5_.refs_0_, bf16[512,2688]{1,0:T(8,128)(2,1)} %shard_map.185.refs_5_.refs_1_, bf16[5504,8192]{1,0:T(8,128)(2,1)} %refs_2_.7, ...), custom_call_target="tpu_custom_call" | custom-call | tf_op jit(solution)/shard_map/pallas_call | solution.py:200
  664.3 19.7 %shard_map.190 = (bf16[128,2048]{1,0:T(8,128)(2,1)}, bf16[128,2048]{1,0:T(8,128)(2,1)}, bf16[128,2048]{1,0:T(8,128)(2,1)}, bf16[128,2048]{1,0:T(8,128)(2,1)}) custom-call(bf16[512,2816]{1,0:T(8,128)(2,1)} %shard_map.183.refs_5_.refs_0_, bf16[512,2688]{1,0:T(8,128)(2,1)} %shard_map.185.refs_5_.refs_1_, bf16[5504,8192]{1,0:T(8,128)(2,1)} %refs_2_.7, ...), custom_call_target="tpu_custom_call" | custom-call | tf_op jit(solution)/shard_map/pallas_call | solution.py:200
  692.5 9.8 %collective-permute-done.48.refs_1_ = bf16[128,2048]{1,0:T(8,128)(2,1)S(1)} collective-permute-done((bf16[128,2048]{1,0:T(8,128)(2,1)}, bf16[128,2048]{1,0:T(8,128)(2,1)S(1)}, u32[]{:S(2)}, u32[]{:S(2)}) %collective-permute-start.48) | collective-permute-done | bytes 524320 | tf_op jit(solution)/shard_map/ppermute | solution.py:333
  703.2 10.4 %collective-permute-done.38.refs_0_ = bf16[128,2048]{1,0:T(8,128)(2,1)} collective-permute-done((bf16[128,2048]{1,0:T(8,128)(2,1)}, bf16[128,2048]{1,0:T(8,128)(2,1)}, u32[]{:S(2)}, u32[]{:S(2)}) %collective-permute-start.38) | collective-permute-done | bytes 524320 | tf_op jit(solution)/shard_map/ppermute | solution.py:333
  726.5 7.4 shard_map.195
  739.2 7.4 shard_map.198
  752.1 7.4 collective-permute-done.31.refs_2_
  767.5 4.5 collective-permute-done.54.refs_0_
  772.5 10.0 %collective-permute-done.53.refs_0_ = bf16[128,2048]{1,0:T(8,128)(2,1)} collective-permute-done((bf16[128,2048]{1,0:T(8,128)(2,1)}, bf16[128,2048]{1,0:T(8,128)(2,1)}, u32[]{:S(2)}, u32[]{:S(2)}) %collective-permute-start.53) | collective-permute-done | bytes 524320 | tf_op jit(solution)/shard_map/ppermute | solution.py:333
  (157 shorter events, 83.6 us)
Async XLA Ops:
  61.2 47.2 %collective-permute-start.4 = (bf16[64,4096]{1,0:T(8,128)(2,1)}, bf16[64,4096]{1,0:T(8,128)(2,1)}, u32[]{:S(2)}, u32[]{:S(2)}) collective-permute-start(bf16[64,4096]{1,0:T(8,128)(2,1)} %get-tuple-element.80), channel_id=1, source_target_pairs={{0,3},{1,2},{2,1},{3,0},{4,7},{5,6},{6,5},{7,4},{8,11},{9,10},{10,... | collective-permute-start | bytes 1572872 | tf_op jit(solution)/shard_map/ppermute | solution.py:333
  61.2 47.2 %collective-permute-start.5 = (bf16[64,4096]{1,0:T(8,128)(2,1)}, bf16[64,4096]{1,0:T(8,128)(2,1)}, u32[]{:S(2)}, u32[]{:S(2)}) collective-permute-start(bf16[64,4096]{1,0:T(8,128)(2,1)} %get-tuple-element.81), channel_id=1, source_target_pairs={{0,1},{1,0},{2,3},{3,2},{4,5},{5,4},{6,7},{7,6},{8,9},{9,8},{10,11... | collective-permute-start | bytes 1572872 | tf_op jit(solution)/shard_map/ppermute | solution.py:333
  61.3 47.1 %collective-permute-start = (bf16[64,4096]{1,0:T(8,128)(2,1)}, bf16[64,4096]{1,0:T(8,128)(2,1)}, u32[]{:S(2)}, u32[]{:S(2)}) collective-permute-start(bf16[64,4096]{1,0:T(8,128)(2,1)} %get-tuple-element.76), channel_id=1, source_target_pairs={{0,2},{1,3},{2,0},{3,1},{4,6},{5,7},{6,4},{7,5},{8,10},{9,11},{10,... | collective-permute-start | bytes 1572872 | tf_op jit(solution)/shard_map/ppermute | solution.py:333
  63.3 45.1 %collective-permute-start.1 = (bf16[64,4096]{1,0:T(8,128)(2,1)}, bf16[64,4096]{1,0:T(8,128)(2,1)}, u32[]{:S(2)}, u32[]{:S(2)}) collective-permute-start(bf16[64,4096]{1,0:T(8,128)(2,1)} %get-tuple-element.77), channel_id=1, source_target_pairs={{0,3},{1,2},{2,1},{3,0},{4,7},{5,6},{6,5},{7,4},{8,11},{9,10},{10,... | collective-permute-start | bytes 1572872 | tf_op jit(solution)/shard_map/ppermute | solution.py:333
  74.2 34.3 %collective-permute-start.2 = (bf16[64,4096]{1,0:T(8,128)(2,1)}, bf16[64,4096]{1,0:T(8,128)(2,1)}, u32[]{:S(2)}, u32[]{:S(2)}) collective-permute-start(bf16[64,4096]{1,0:T(8,128)(2,1)} %get-tuple-element.78), channel_id=1, source_target_pairs={{0,1},{1,0},{2,3},{3,2},{4,5},{5,4},{6,7},{7,6},{8,9},{9,8},{10,11... | collective-permute-start | bytes 1572872 | tf_op jit(solution)/shard_map/ppermute | solution.py:333
  131.4 63.5 %collective-permute-start.7 = (bf16[64,8192]{1,0:T(8,128)(2,1)}, bf16[64,8192]{1,0:T(8,128)(2,1)}, u32[]{:S(2)}, u32[]{:S(2)}) collective-permute-start(bf16[64,8192]{1,0:T(8,128)(2,1)} %get-tuple-element.85), channel_id=1, source_target_pairs={{0,2},{1,3},{2,0},{3,1},{4,6},{5,7},{6,4},{7,5},{8,10},{9,11},{10,... | collective-permute-start | bytes 3145736 | tf_op jit(solution)/shard_map/ppermute | solution.py:333
  133.5 61.4 %collective-permute-start.8 = (bf16[64,8192]{1,0:T(8,128)(2,1)}, bf16[64,8192]{1,0:T(8,128)(2,1)}, u32[]{:S(2)}, u32[]{:S(2)}) collective-permute-start(bf16[64,8192]{1,0:T(8,128)(2,1)} %get-tuple-element.86), channel_id=1, source_target_pairs={{0,3},{1,2},{2,1},{3,0},{4,7},{5,6},{6,5},{7,4},{8,11},{9,10},{10,... | collective-permute-start | bytes 3145736 | tf_op jit(solution)/shard_map/ppermute | solution.py:333
  133.6 61.3 %collective-permute-start.9 = (bf16[64,8192]{1,0:T(8,128)(2,1)}, bf16[64,8192]{1,0:T(8,128)(2,1)}, u32[]{:S(2)}, u32[]{:S(2)}) collective-permute-start(bf16[64,8192]{1,0:T(8,128)(2,1)} %get-tuple-element.87), channel_id=1, source_target_pairs={{0,1},{1,0},{2,3},{3,2},{4,5},{5,4},{6,7},{7,6},{8,9},{9,8},{10,11... | collective-permute-start | bytes 3145736 | tf_op jit(solution)/shard_map/ppermute | solution.py:333
  133.7 69.0 %collective-permute-start.6 = (bf16[64,8192]{1,0:T(8,128)(2,1)}, bf16[64,8192]{1,0:T(8,128)(2,1)}, u32[]{:S(2)}, u32[]{:S(2)}) collective-permute-start(bf16[64,8192]{1,0:T(8,128)(2,1)} %get-tuple-element.82.refs_2_.refs_0_), channel_id=1, source_target_pairs={{0,2},{1,3},{2,0},{3,1},{4,6},{5,7},{6,4},{7,5},{8,10},{9,11},{10,... | collective-permute-start | bytes 3145736 | tf_op jit(solution)/shard_map/ppermute | solution.py:333
  199.6 35.3 %collective-permute-start.18 = (bf16[64,8192]{1,0:T(8,128)(2,1)}, bf16[64,8192]{1,0:T(8,128)(2,1)}, u32[]{:S(2)}, u32[]{:S(2)}) collective-permute-start(bf16[64,8192]{1,0:T(8,128)(2,1)} %get-tuple-element.89.refs_1_), channel_id=1, source_target_pairs={{0,2},{1,3},{2,0},{3,1},{4,6},{5,7},{6,4},{7,5},{8,10},{9,11},{10,... | collective-permute-start | bytes 3145736 | tf_op jit(solution)/shard_map/ppermute | solution.py:333
  199.6 35.3 %collective-permute-start.16 = (bf16[64,8192]{1,0:T(8,128)(2,1)}, bf16[64,8192]{1,0:T(8,128)(2,1)}, u32[]{:S(2)}, u32[]{:S(2)}) collective-permute-start(bf16[64,8192]{1,0:T(8,128)(2,1)} %get-tuple-element.82.refs_2_.refs_0_), channel_id=1, source_target_pairs={{0,1},{1,0},{2,3},{3,2},{4,5},{5,4},{6,7},{7,6},{8,9},{9,8},{10,11... | collective-permute-start | bytes 3145736 | tf_op jit(solution)/shard_map/ppermute | solution.py:333
  234.9 135.8 %collective-permute-start.14 = (bf16[128,4096]{1,0:T(8,128)(2,1)}, bf16[128,4096]{1,0:T(8,128)(2,1)}, u32[]{:S(2)}, u32[]{:S(2)}) collective-permute-start(bf16[128,4096]{1,0:T(8,128)(2,1)} %get-tuple-element.96), channel_id=1, source_target_pairs={{0,3},{1,2},{2,1},{3,0},{4,7},{5,6},{6,5},{7,4},{8,11},{9,10},{10,... | collective-permute-start | bytes 3145736 | tf_op jit(solution)/shard_map/ppermute | solution.py:333
  235.1 135.6 %collective-permute-start.15 = (bf16[128,4096]{1,0:T(8,128)(2,1)}, bf16[128,4096]{1,0:T(8,128)(2,1)}, u32[]{:S(2)}, u32[]{:S(2)}) collective-permute-start(bf16[128,4096]{1,0:T(8,128)(2,1)} %get-tuple-element.97), channel_id=1, source_target_pairs={{0,1},{1,0},{2,3},{3,2},{4,5},{5,4},{6,7},{7,6},{8,9},{9,8},{10,11... | collective-permute-start | bytes 3145736 | tf_op jit(solution)/shard_map/ppermute | solution.py:333
  235.5 135.2 %collective-permute-start.10 = (bf16[128,4096]{1,0:T(8,128)(2,1)}, bf16[128,4096]{1,0:T(8,128)(2,1)}, u32[]{:S(2)}, u32[]{:S(2)}) collective-permute-start(bf16[128,4096]{1,0:T(8,128)(2,1)} %get-tuple-element.91), channel_id=1, source_target_pairs={{0,2},{1,3},{2,0},{3,1},{4,6},{5,7},{6,4},{7,5},{8,10},{9,11},{10,... | collective-permute-start | bytes 3145736 | tf_op jit(solution)/shard_map/ppermute | solution.py:333
  259.2 111.5 %collective-permute-start.11 = (bf16[128,4096]{1,0:T(8,128)(2,1)}, bf16[128,4096]{1,0:T(8,128)(2,1)}, u32[]{:S(2)}, u32[]{:S(2)}) collective-permute-start(bf16[128,4096]{1,0:T(8,128)(2,1)} %get-tuple-element.92), channel_id=1, source_target_pairs={{0,3},{1,2},{2,1},{3,0},{4,7},{5,6},{6,5},{7,4},{8,11},{9,10},{10,... | collective-permute-start | bytes 3145736 | tf_op jit(solution)/shard_map/ppermute | solution.py:333
  259.2 111.5 %collective-permute-start.12 = (bf16[128,4096]{1,0:T(8,128)(2,1)}, bf16[128,4096]{1,0:T(8,128)(2,1)}, u32[]{:S(2)}, u32[]{:S(2)}) collective-permute-start(bf16[128,4096]{1,0:T(8,128)(2,1)} %get-tuple-element.93), channel_id=1, source_target_pairs={{0,1},{1,0},{2,3},{3,2},{4,5},{5,4},{6,7},{7,6},{8,9},{9,8},{10,11... | collective-permute-start | bytes 3145736 | tf_op jit(solution)/shard_map/ppermute | solution.py:333
  378.0 64.4 %collective-permute-start.22 = (bf16[128,8192]{1,0:T(8,128)(2,1)}, bf16[128,8192]{1,0:T(8,128)(2,1)}, u32[]{:S(2)}, u32[]{:S(2)}) collective-permute-start(bf16[128,8192]{1,0:T(8,128)(2,1)} %get-tuple-element.98.refs_2_.refs_0_), channel_id=1, source_target_pairs={{0,2},{1,3},{2,0},{3,1},{4,6},{5,7},{6,4},{7,5},{8,10},{9,11},{10,... | collective-permute-start | bytes 6291464 | tf_op jit(solution)/shard_map/ppermute | solution.py:333
  378.0 93.2 %collective-permute-start.21 = (bf16[128,8192]{1,0:T(8,128)(2,1)}, bf16[128,8192]{1,0:T(8,128)(2,1)}, u32[]{:S(2)}, u32[]{:S(2)}) collective-permute-start(bf16[128,8192]{1,0:T(8,128)(2,1)} %get-tuple-element.98.refs_2_.refs_0_), channel_id=1, source_target_pairs={{0,1},{1,0},{2,3},{3,2},{4,5},{5,4},{6,7},{7,6},{8,9},{9,8},{10,11... | collective-permute-start | bytes 6291464 | tf_op jit(solution)/shard_map/ppermute | solution.py:333
  444.8 85.8 %collective-permute-start.25 = (bf16[128,4096]{1,0:T(8,128)(2,1)}, bf16[128,4096]{1,0:T(8,128)(2,1)}, u32[]{:S(2)}, u32[]{:S(2)}) collective-permute-start(bf16[128,4096]{1,0:T(8,128)(2,1)} %get-tuple-element.102), channel_id=1, source_target_pairs={{0,3},{1,2},{2,1},{3,0},{4,7},{5,6},{6,5},{7,4},{8,11},{9,10},{10,... | collective-permute-start | bytes 3145736 | tf_op jit(solution)/shard_map/ppermute | solution.py:333
  444.8 85.8 %collective-permute-start.26 = (bf16[128,4096]{1,0:T(8,128)(2,1)}, bf16[128,4096]{1,0:T(8,128)(2,1)}, u32[]{:S(2)}, u32[]{:S(2)}) collective-permute-start(bf16[128,4096]{1,0:T(8,128)(2,1)} %get-tuple-element.103), channel_id=1, source_target_pairs={{0,1},{1,0},{2,3},{3,2},{4,5},{5,4},{6,7},{7,6},{8,9},{9,8},{10,11... | collective-permute-start | bytes 3145736 | tf_op jit(solution)/shard_map/ppermute | solution.py:333
  469.2 126.2 %collective-permute-start.27 = (bf16[128,4096]{1,0:T(8,128)(2,1)}, bf16[128,4096]{1,0:T(8,128)(2,1)}, u32[]{:S(2)}, u32[]{:S(2)}) collective-permute-start(bf16[128,4096]{1,0:T(8,128)(2,1)} %get-tuple-element.105), channel_id=1, source_target_pairs={{0,2},{1,3},{2,0},{3,1},{4,6},{5,7},{6,4},{7,5},{8,10},{9,11},{10,... | collective-permute-start | bytes 3145736 | tf_op jit(solution)/shard_map/ppermute | solution.py:333
  471.2 124.2 %collective-permute-start.28 = (bf16[128,4096]{1,0:T(8,128)(2,1)}, bf16[128,4096]{1,0:T(8,128)(2,1)}, u32[]{:S(2)}, u32[]{:S(2)}) collective-permute-start(bf16[128,4096]{1,0:T(8,128)(2,1)} %get-tuple-element.106), channel_id=1, source_target_pairs={{0,3},{1,2},{2,1},{3,0},{4,7},{5,6},{6,5},{7,4},{8,11},{9,10},{10,... | collective-permute-start | bytes 3145736 | tf_op jit(solution)/shard_map/ppermute | solution.py:333
  471.2 124.2 %collective-permute-start.29 = (bf16[128,4096]{1,0:T(8,128)(2,1)}, bf16[128,4096]{1,0:T(8,128)(2,1)}, u32[]{:S(2)}, u32[]{:S(2)}) collective-permute-start(bf16[128,4096]{1,0:T(8,128)(2,1)} %get-tuple-element.107), channel_id=1, source_target_pairs={{0,1},{1,0},{2,3},{3,2},{4,5},{5,4},{6,7},{7,6},{8,9},{9,8},{10,11... | collective-permute-start | bytes 3145736 | tf_op jit(solution)/shard_map/ppermute | solution.py:333
  534.2 110.5 %collective-permute-start.36 = (bf16[128,4096]{1,0:T(8,128)(2,1)}, bf16[128,4096]{1,0:T(8,128)(2,1)}, u32[]{:S(2)}, u32[]{:S(2)}) collective-permute-start(bf16[128,4096]{1,0:T(8,128)(2,1)} %shard_map.184.refs_6_.refs_1_), channel_id=1, source_target_pairs={{0,2},{1,3},{2,0},{3,1},{4,6},{5,7},{6,4},{7,5},{8,10},{9,11},{10,... | collective-permute-start | bytes 3145736 | tf_op jit(solution)/shard_map/ppermute | solution.py:333
  620.6 71.3 %collective-permute-start.44 = (bf16[128,4096]{1,0:T(8,128)(2,1)}, bf16[128,4096]{1,0:T(8,128)(2,1)}, u32[]{:S(2)}, u32[]{:S(2)}) collective-permute-start(bf16[128,4096]{1,0:T(8,128)(2,1)} %shard_map.186.refs_3_.refs_1_), channel_id=1, source_target_pairs={{0,2},{1,3},{2,0},{3,1},{4,6},{5,7},{6,4},{7,5},{8,10},{9,11},{10,... | collective-permute-start | bytes 3145736 | tf_op jit(solution)/shard_map/ppermute | solution.py:333
  641.0 43.0 %collective-permute-start.41 = (bf16[128,2048]{1,0:T(8,128)(2,1)}, bf16[128,2048]{1,0:T(8,128)(2,1)S(1)}, u32[]{:S(2)}, u32[]{:S(2)}) collective-permute-start(bf16[128,2048]{1,0:T(8,128)(2,1)} %get-tuple-element.119), channel_id=1, source_target_pairs={{0,2},{1,3},{2,0},{3,1},{4,6},{5,7},{6,4},{7,5},{8,10},{9,11},{10,... | collective-permute-start | bytes 1572872 | tf_op jit(solution)/shard_map/ppermute | solution.py:333
  643.0 44.3 %collective-permute-start.42 = (bf16[128,2048]{1,0:T(8,128)(2,1)}, bf16[128,2048]{1,0:T(8,128)(2,1)}, u32[]{:S(2)}, u32[]{:S(2)}) collective-permute-start(bf16[128,2048]{1,0:T(8,128)(2,1)} %get-tuple-element.120), channel_id=1, source_target_pairs={{0,3},{1,2},{2,1},{3,0},{4,7},{5,6},{6,5},{7,4},{8,11},{9,10},{10,... | collective-permute-start | bytes 1572872 | tf_op jit(solution)/shard_map/ppermute | solution.py:333
  644.3 58.3 %collective-permute-start.39 = (bf16[128,4096]{1,0:T(8,128)(2,1)}, bf16[128,4096]{1,0:T(8,128)(2,1)}, u32[]{:S(2)}, u32[]{:S(2)}) collective-permute-start(bf16[128,4096]{1,0:T(8,128)(2,1)} %shard_map.184.refs_6_.refs_1_), channel_id=1, source_target_pairs={{0,1},{1,0},{2,3},{3,2},{4,5},{5,4},{6,7},{7,6},{8,9},{9,8},{10,11... | collective-permute-start | bytes 3145736 | tf_op jit(solution)/shard_map/ppermute | solution.py:333
  644.7 46.0 %collective-permute-start.43 = (bf16[128,2048]{1,0:T(8,128)(2,1)}, bf16[128,2048]{1,0:T(8,128)(2,1)}, u32[]{:S(2)}, u32[]{:S(2)}) collective-permute-start(bf16[128,2048]{1,0:T(8,128)(2,1)} %get-tuple-element.121), channel_id=1, source_target_pairs={{0,1},{1,0},{2,3},{3,2},{4,5},{5,4},{6,7},{7,6},{8,9},{9,8},{10,11... | collective-permute-start | bytes 1572872 | tf_op jit(solution)/shard_map/ppermute | solution.py:333
  684.1 32.2 %collective-permute-start.40 = (bf16[128,4096]{1,0:T(8,128)(2,1)}, bf16[128,4096]{1,0:T(8,128)(2,1)}, u32[]{:S(2)}, u32[]{:S(2)}) collective-permute-start(bf16[128,4096]{1,0:T(8,128)(2,1)} %shard_map.191.refs_5_.refs_3_), channel_id=1, source_target_pairs={{0,1},{1,0},{2,3},{3,2},{4,5},{5,4},{6,7},{7,6},{8,9},{9,8},{10,11... | collective-permute-start | bytes 3145736 | tf_op jit(solution)/shard_map/ppermute | solution.py:333
  692.0 42.4 %collective-permute-start.46 = (bf16[128,4096]{1,0:T(8,128)(2,1)}, bf16[128,4096]{1,0:T(8,128)(2,1)}, u32[]{:S(2)}, u32[]{:S(2)}) collective-permute-start(bf16[128,4096]{1,0:T(8,128)(2,1)} %shard_map.186.refs_3_.refs_1_), channel_id=1, source_target_pairs={{0,1},{1,0},{2,3},{3,2},{4,5},{5,4},{6,7},{7,6},{8,9},{9,8},{10,11... | collective-permute-start | bytes 3145736 | tf_op jit(solution)/shard_map/ppermute | solution.py:333
  702.3 33.7 %collective-permute-start.47 = (bf16[128,4096]{1,0:T(8,128)(2,1)}, bf16[128,4096]{1,0:T(8,128)(2,1)}, u32[]{:S(2)}, u32[]{:S(2)}) collective-permute-start(bf16[128,4096]{1,0:T(8,128)(2,1)} %shard_map.193.refs_5_.refs_3_), channel_id=1, source_target_pairs={{0,1},{1,0},{2,3},{3,2},{4,5},{5,4},{6,7},{7,6},{8,9},{9,8},{10,11... | collective-permute-start | bytes 3145736 | tf_op jit(solution)/shard_map/ppermute | solution.py:333
  (38 other events, 713.5 us)
